TPU v7x, 32 devices: a whole 2x2x4 slice. The times are simulated.
32 devices in a mesh: gx: 4 (over y, core), gy: 4 (over z), gz: 2 (over x).
Axes of the slice: x: 2, y: 2, z: 4, core: 2. Of those that a mesh axis runs over, the one named last changes fastest.
Arguments:
- rhs: float32 [4, 32, 32, 256], P(None, 'gx', 'gy', 'gz'), may hold values from -170 to 170
- basis: bfloat16 [4, 8, 32, 32, 256], P(None, None, 'gx', 'gy', 'gz'), may hold values from -6 to 6
- inertia: float32 [32, 32, 256], P('gx', 'gy', 'gz'), may hold values from 0.5 to 2
- helm: float32 [4], replicated, may hold values from 0.2 to 1
- stiffness: float32 [8, 8], replicated, may hold values from -0.05 to 0.6, as said below
Outputs:
- solution: float32 [4, 32, 32, 256], P(None, 'gx', 'gy', 'gz')
- new_basis: bfloat16 [4, 32, 32, 256], P(None, 'gx', 'gy', 'gz')
Inputs may be any that keep to these rules, and one draw needn't show every extreme that they name: `stiffness`: symmetric; every diagonal entry exceeds the sum of the magnitudes of the other entries of its row.
All inputs are finite; a program needn't handle non-finite values.
Results may differ from a plain program's by a relative error of at most 0.001.
Values sent between devices are 32-bit elements; how exact they have to be, the bound alone decides.
A program may use at most 64 MiB of HBM per device.

v0:
```python
import jax
import jax.numpy as jnp
from jax import lax
from jax.sharding import PartitionSpec as P

ITERS = 2
penalty = 0.15
epsilon = 1e-06
highest = lax.Precision.HIGHEST


def padded_2(block, sides, width):
    for axis, dim in sides:
        count = lax.axis_size(axis)
        forward = [(i, i + 1) for i in range(count - 1)]
        backward = [(target, source) for source, target in forward]
        low = lax.ppermute(
            lax.slice_in_dim(block, block.shape[dim] - width, None, axis=dim), axis, forward
        )
        high = lax.ppermute(lax.slice_in_dim(block, 0, width, axis=dim), axis, backward)
        block = jnp.concatenate([low, block, high], axis=dim)
    return block


def block_matrix(stiffness, size_c):
    points = stiffness.shape[0]
    cells = lax.broadcasted_iota(jnp.int32, (size_c, points), 0)
    slots = lax.broadcasted_iota(jnp.int32, (size_c, points), 1)
    selector = jnp.where(cells % points == slots, 1.0, 0.0).astype(jnp.float32)
    spread_out = jnp.dot(
        jnp.dot(selector, stiffness, precision=highest), selector.T, precision=highest
    )
    rows_block = lax.broadcasted_iota(jnp.int32, (size_c, size_c), 0) // points
    cols_block = lax.broadcasted_iota(jnp.int32, (size_c, size_c), 1) // points
    return jnp.where(rows_block == cols_block, spread_out, 0.0)


def stiffen(vector, stiffness, full_block):
    leading, size_a, size_b, size_c = vector.shape
    points = stiffness.shape[0]
    along_a = jnp.einsum(
        "ij,sajbc->saibc",
        stiffness,
        vector.reshape(leading, size_a // points, points, size_b, size_c),
        precision=highest,
    ).reshape(vector.shape)
    along_b = jnp.einsum(
        "ij,sabjc->sabic",
        stiffness,
        vector.reshape(leading, size_a, size_b // points, points, size_c),
        precision=highest,
    ).reshape(vector.shape)
    along_c = jnp.einsum("sabj,ij->sabi", vector, full_block, precision=highest)
    return along_a + along_b + along_c


def face_terms(vector, padded, points):
    accumulated = jnp.zeros_like(vector)
    neighbours = (
        (1, padded[:, 2:, 1:-1, 1:-1], padded[:, :-2, 1:-1, 1:-1]),
        (2, padded[:, 1:-1, 2:, 1:-1], padded[:, 1:-1, :-2, 1:-1]),
        (3, padded[:, 1:-1, 1:-1, 2:], padded[:, 1:-1, 1:-1, :-2]),
    )
    for axis_pos, higher, lower_side in neighbours:
        position = lax.broadcasted_iota(jnp.int32, vector.shape, axis_pos) % points
        accumulated = accumulated + jnp.where(position == points - 1, vector - higher, 0.0)
        accumulated = accumulated + jnp.where(position == 0, vector - lower_side, 0.0)
    return accumulated


def operate(vector, padded, diagonal, stiffness, full_block):
    return (
        diagonal * vector
        + stiffen(vector, stiffness, full_block)
        + penalty * face_terms(vector, padded, stiffness.shape[0])
    )


def per_solve(values):
    return values[:, None, None, None]


def on_device(rhs, basis, inertia, helm, stiffness):
    point_count = float(
        rhs[0].size * lax.axis_size("gx") * lax.axis_size("gy") * lax.axis_size("gz")
    )
    diagonal = helm[:, None, None, None] * inertia[None]
    full_block = block_matrix(stiffness, rhs.shape[3])

    def apply_all(vector):
        padded = padded_2(vector, (("gx", 1), ("gy", 2), ("gz", 3)), 1)
        return operate(vector, padded, diagonal, stiffness, full_block)

    def project(fields):
        return jnp.einsum("skxyz,sxyz->sk", basis, fields, precision=highest)

    def combine(weights):
        return jnp.einsum("sk,skxyz->sxyz", weights, basis, precision=highest)

    local_coef = project(rhs)
    local_gram = jnp.einsum("skxyz,slxyz->skl", basis, basis, preferred_element_type=jnp.float32)
    coef_sum, gram_sum = lax.psum((local_coef, local_gram), ("gx", "gy", "gz"))
    gram_matrix = gram_sum / point_count
    iterate = combine(coef_sum / point_count)
    residual = rhs - apply_all(iterate)
    direction = jnp.zeros_like(rhs)
    image_dir = jnp.zeros_like(rhs)
    norm_old = None
    step_old = None
    final_moment = None
    final_square = None
    for iteration in range(ITERS):
        image_vec = apply_all(residual)
        norm_part = jnp.sum(residual * residual, axis=(1, 2, 3))
        curv_part = jnp.sum(residual * image_vec, axis=(1, 2, 3))
        if iteration < ITERS - 1:
            norm_now, curvature = lax.psum((norm_part, curv_part), ("gx", "gy", "gz"))
        else:
            norm_now, curvature = lax.psum((norm_part, curv_part), ("gx", "gy", "gz"))
        if iteration == 0:
            conjugacy = jnp.zeros_like(norm_now)
            step_size = norm_now / curvature
        else:
            conjugacy = norm_now / norm_old
            step_size = norm_now / (curvature - conjugacy * norm_now / step_old)
        direction = residual + per_solve(conjugacy) * direction
        image_dir = image_vec + per_solve(conjugacy) * image_dir
        iterate = iterate + per_solve(step_size) * direction
        if iteration < ITERS - 1:
            residual = residual - per_solve(step_size) * image_dir
        norm_old = norm_now
        step_old = step_size
    final_moment, final_square = lax.psum(
        (project(iterate), jnp.sum(iterate * iterate, axis=(1, 2, 3))), ("gx", "gy", "gz")
    )
    weights = final_moment / point_count
    square = final_square / point_count
    spread = (
        square
        - 2.0 * jnp.sum(weights * weights, axis=1)
        + jnp.einsum("sk,skl,sl->s", weights, gram_matrix, weights, precision=highest)
    )
    remainder = iterate - combine(weights)
    new_basis = (remainder * per_solve(lax.rsqrt(spread + epsilon))).astype(jnp.bfloat16)
    return (iterate, new_basis)


def solution(mesh):
    placed = (
        P(None, "gx", "gy", "gz"),
        P(None, None, "gx", "gy", "gz"),
        P("gx", "gy", "gz"),
        P(),
        P(),
    )
    return jax.shard_map(
        on_device,
        mesh=mesh,
        in_specs=placed,
        out_specs=(P(None, "gx", "gy", "gz"), P(None, "gx", "gy", "gz")),
        check_vma=False,
    )
```

profile of v0, /device:TPU:0, one launch (start us, length us, event | category | flops | bytes accessed | tf_op | source)
XLA Modules:
  0.0 254.5 jit_solution(11118584132166019880)
XLA Ops:
  0.7 2.6 %fusion.20 = f32[4,1,8,1,1]{2,1,4,3,0:T(1,128)S(1)} fusion(f32[4,8,8,128,1]{3,4,2,1,0:T(1,128)} %bitcast.131, bf16[4,8,8,8,128]{4,3,2,1,0:T(8,128)(2,1)} %param.6), kind=kOutput, calls=%fused_computation.31 | convolution fusion | flops 3145728 | bytes 655488 | tf_op jit(solution)/shard_map/skxyz,sxyz->sk/dot_general | solution.py:95
  3.3 41.9 %psum.56 = f32[4,8]{1,0:T(4,128)S(1)} all-reduce(f32[4,8]{1,0:T(4,128)S(1)} %bitcast.130), channel_id=1, replica_groups=mesh['gx'=4,'gy'=4,'gz'=2] {'gx','gy','gz'}, use_global_device_ids=true, to_apply=%region_0.1 | all-reduce | flops 32 | bytes 256 | tf_op jit(solution)/shard_map/psum | solution.py:102
  46.0 1.3 collective-permute-start
  47.3 3.0 %collective-permute-start.1 = (f32[4,1,8,128]{3,1,2,0:T(1,128)S(1)}, f32[4,1,8,128]{3,1,2,0:T(1,128)S(1)}, u32[]{:S(2)}, u32[]{:S(2)}) collective-permute-start(f32[4,1,8,128]{3,1,2,0:T(1,128)S(1)} %get-tuple-element.39), channel_id=1, source_target_pairs={{0,8},{8,16},{16,24},{1,9},{9,17},{17,25},{2,10},{10,18},{18,26},{... | collective-permute-start | bytes 49160 | tf_op jit(solution)/shard_map/ppermute | solution.py:17
  51.6 1.3 collective-permute-start.2
  52.9 4.5 %collective-permute-start.3 = (f32[4,10,1,128]{3,1,2,0:T(8,128)S(1)}, f32[4,10,1,128]{3,1,2,0:T(8,128)S(1)}, u32[]{:S(2)}, u32[]{:S(2)}) collective-permute-start(f32[4,10,1,128]{3,1,2,0:T(8,128)S(1)} %get-tuple-element.33), channel_id=1, source_target_pairs={{0,2},{2,4},{4,6},{1,3},{3,5},{5,7},{8,10},{10,12},{12,14},{9,11},... | collective-permute-start | bytes 61448 | tf_op jit(solution)/shard_map/ppermute | solution.py:17
  57.5 1.6 collective-permute-done.3
  60.6 4.6 %collective-permute-start.5 = (f32[4,10,10,1]{3,1,2,0:T(8,128)S(1)}, f32[4,10,10,1]{3,1,2,0:T(8,128)S(1)}, u32[]{:S(2)}, u32[]{:S(2)}) collective-permute-start(f32[4,10,10,1]{3,1,2,0:T(8,128)S(1)} %get-tuple-element.28), channel_id=1, source_target_pairs={{0,1},{2,3},{4,5},{6,7},{8,9},{10,11},{12,13},{14,15},{16,17},{18,... | collective-permute-start | bytes 4808 | tf_op jit(solution)/shard_map/ppermute | solution.py:17
  65.2 6.3 %collective-permute-done.4 = f32[4,10,10,1]{3,1,2,0:T(8,128)S(1)} collective-permute-done((f32[4,10,10,1]{3,1,2,0:T(8,128)S(1)}, f32[4,10,10,1]{3,1,2,0:T(8,128)S(1)}, u32[]{:S(2)}, u32[]{:S(2)}) %collective-permute-start.4) | collective-permute-done | bytes 1632 | tf_op jit(solution)/shard_map/ppermute | solution.py:20
  75.1 3.0 %collective-permute-start.7 = (f32[4,1,8,128]{3,1,2,0:T(1,128)S(1)}, f32[4,1,8,128]{3,1,2,0:T(1,128)S(1)}, u32[]{:S(2)}, u32[]{:S(2)}) collective-permute-start(f32[4,1,8,128]{3,1,2,0:T(1,128)S(1)} %get-tuple-element.37), channel_id=1, source_target_pairs={{0,8},{8,16},{16,24},{1,9},{9,17},{17,25},{2,10},{10,18},{18,26},{... | collective-permute-start | bytes 49160 | tf_op jit(solution)/shard_map/ppermute | solution.py:17
  80.3 4.6 %collective-permute-start.9 = (f32[4,10,1,128]{3,1,2,0:T(8,128)S(1)}, f32[4,10,1,128]{3,1,2,0:T(8,128)S(1)}, u32[]{:S(2)}, u32[]{:S(2)}) collective-permute-start(f32[4,10,1,128]{3,1,2,0:T(8,128)S(1)} %get-tuple-element.31), channel_id=1, source_target_pairs={{0,2},{2,4},{4,6},{1,3},{3,5},{5,7},{8,10},{10,12},{12,14},{9,11},... | collective-permute-start | bytes 61448 | tf_op jit(solution)/shard_map/ppermute | solution.py:17
  85.1 1.3 collective-permute-done.9
  88.0 4.6 %collective-permute-start.11 = (f32[4,10,10,1]{3,1,2,0:T(8,128)S(1)}, f32[4,10,10,1]{3,1,2,0:T(8,128)S(1)}, u32[]{:S(2)}, u32[]{:S(2)}) collective-permute-start(f32[4,10,10,1]{3,1,2,0:T(8,128)S(1)} %get-tuple-element.26), channel_id=1, source_target_pairs={{0,1},{2,3},{4,5},{6,7},{8,9},{10,11},{12,13},{14,15},{16,17},{18,... | collective-permute-start | bytes 4808 | tf_op jit(solution)/shard_map/ppermute | solution.py:17
  92.8 5.2 %collective-permute-done.10 = f32[4,10,10,1]{3,1,2,0:T(8,128)S(1)} collective-permute-done((f32[4,10,10,1]{3,1,2,0:T(8,128)S(1)}, f32[4,10,10,1]{3,1,2,0:T(8,128)S(1)}, u32[]{:S(2)}, u32[]{:S(2)}) %collective-permute-start.10) | collective-permute-done | bytes 1632 | tf_op jit(solution)/shard_map/ppermute | solution.py:20
  99.7 41.8 %all-reduce.2 = (f32[4]{0:T(128)S(1)}, f32[4]{0:T(128)S(1)}) all-reduce(f32[4]{0:T(128)S(1)} %get-tuple-element.7, f32[4]{0:T(128)S(1)} %get-tuple-element.6), channel_id=1, replica_groups=mesh['gx'=4,'gy'=4,'gz'=2] {'gx','gy','gz'}, use_global_device_ids=true, to_apply=%region_2.3 | all-reduce | flops 8 | bytes 64 | tf_op jit(solution)/shard_map/psum | solution.py:117
  143.0 3.0 %collective-permute-start.13 = (f32[4,1,8,128]{3,1,2,0:T(1,128)S(1)}, f32[4,1,8,128]{3,1,2,0:T(1,128)S(1)}, u32[]{:S(2)}, u32[]{:S(2)}) collective-permute-start(f32[4,1,8,128]{3,1,2,0:T(1,128)S(1)} %get-tuple-element.35), channel_id=1, source_target_pairs={{0,8},{8,16},{16,24},{1,9},{9,17},{17,25},{2,10},{10,18},{18,26},{... | collective-permute-start | bytes 49160 | tf_op jit(solution)/shard_map/ppermute | solution.py:17
  146.9 1.3 collective-permute-start.14
  148.2 4.5 %collective-permute-start.15 = (f32[4,10,1,128]{3,1,2,0:T(8,128)S(1)}, f32[4,10,1,128]{3,1,2,0:T(8,128)S(1)}, u32[]{:S(2)}, u32[]{:S(2)}) collective-permute-start(f32[4,10,1,128]{3,1,2,0:T(8,128)S(1)} %get-tuple-element.29), channel_id=1, source_target_pairs={{0,2},{2,4},{4,6},{1,3},{3,5},{5,7},{8,10},{10,12},{12,14},{9,11},... | collective-permute-start | bytes 61448 | tf_op jit(solution)/shard_map/ppermute | solution.py:17
  153.0 1.3 collective-permute-done.15
  155.9 4.6 %collective-permute-start.17 = (f32[4,10,10,1]{3,1,2,0:T(8,128)S(1)}, f32[4,10,10,1]{3,1,2,0:T(8,128)S(1)}, u32[]{:S(2)}, u32[]{:S(2)}) collective-permute-start(f32[4,10,10,1]{3,1,2,0:T(8,128)S(1)} %get-tuple-element.24), channel_id=1, source_target_pairs={{0,1},{2,3},{4,5},{6,7},{8,9},{10,11},{12,13},{14,15},{16,17},{18,... | collective-permute-start | bytes 4808 | tf_op jit(solution)/shard_map/ppermute | solution.py:17
  160.7 6.1 %collective-permute-done.16 = f32[4,10,10,1]{3,1,2,0:T(8,128)S(1)} collective-permute-done((f32[4,10,10,1]{3,1,2,0:T(8,128)S(1)}, f32[4,10,10,1]{3,1,2,0:T(8,128)S(1)}, u32[]{:S(2)}, u32[]{:S(2)}) %collective-permute-start.16) | collective-permute-done | bytes 1632 | tf_op jit(solution)/shard_map/ppermute | solution.py:20
  168.5 41.5 %all-reduce.1 = (f32[4]{0:T(128)S(1)}, f32[4]{0:T(128)S(1)}) all-reduce(f32[4]{0:T(128)S(1)} %get-tuple-element.21, f32[4]{0:T(128)S(1)} %fusion.11), channel_id=1, replica_groups=mesh['gx'=4,'gy'=4,'gz'=2] {'gx','gy','gz'}, use_global_device_ids=true, to_apply=%region_6.7 | all-reduce | flops 8 | bytes 64 | tf_op jit(solution)/shard_map/psum | solution.py:119
  211.0 1.6 fusion.16
  212.6 40.1 %all-reduce = (f32[4,8]{1,0:T(4,128)S(1)}, f32[4,8,8]{2,1,0:T(8,128)S(1)}, f32[4]{0:T(128)S(1)}) all-reduce(f32[4,8]{1,0:T(4,128)S(1)} %bitcast.129, f32[4,8,8]{2,1,0:T(8,128)S(1)} %convolution_bitcast_fusion.3, f32[4]{0:T(128)S(1)} %get-tuple-element.17), channel_id=1, replica_groups=mesh['gx'=4,'gy'=4,'gz'=2] {'gx','gy','gz'}, use_global_device_ids=true, to_apply=%region_9.10 | all-reduce | flops 292 | bytes 2336 | tf_op jit(solution)/shard_map/psum | solution.py:133
  (74 shorter events, 21.6 us)
Async XLA Ops:
  0.6 49.8 %copy-start = (f32[8,8]{1,0:T(8,128)S(1)}, f32[8,8]{1,0:T(8,128)}, u32[]{:S(2)}) copy-start(f32[8,8]{1,0:T(8,128)} %param.9) | copy-start | bytes 772
  0.6 44.6 %copy-start.1 = (bf16[4,8,8,8,128]{4,3,2,1,0:T(8,128)(2,1)S(1)}, bf16[4,8,8,8,128]{4,3,2,1,0:T(8,128)(2,1)}, u32[]{:S(2)}) copy-start(bf16[4,8,8,8,128]{4,3,2,1,0:T(8,128)(2,1)} %param.6) | copy-start | bytes 1572868
  46.0 5.6 %collective-permute-start = (f32[4,1,8,128]{3,1,2,0:T(1,128)S(1)}, f32[4,1,8,128]{3,1,2,0:T(1,128)S(1)}, u32[]{:S(2)}, u32[]{:S(2)}) collective-permute-start(f32[4,1,8,128]{3,1,2,0:T(1,128)S(1)} %get-tuple-element.40), channel_id=1, source_target_pairs={{8,0},{16,8},{24,16},{9,1},{17,9},{25,17},{10,2},{18,10},{26,18},{... | collective-permute-start | bytes 49160 | tf_op jit(solution)/shard_map/ppermute | solution.py:20
  47.3 4.3 %collective-permute-start.1 = (f32[4,1,8,128]{3,1,2,0:T(1,128)S(1)}, f32[4,1,8,128]{3,1,2,0:T(1,128)S(1)}, u32[]{:S(2)}, u32[]{:S(2)}) collective-permute-start(f32[4,1,8,128]{3,1,2,0:T(1,128)S(1)} %get-tuple-element.39), channel_id=1, source_target_pairs={{0,8},{8,16},{16,24},{1,9},{9,17},{17,25},{2,10},{10,18},{18,26},{... | collective-permute-start | bytes 49160 | tf_op jit(solution)/shard_map/ppermute | solution.py:17
  51.6 5.9 %collective-permute-start.2 = (f32[4,10,1,128]{3,1,2,0:T(8,128)S(1)}, f32[4,10,1,128]{3,1,2,0:T(8,128)S(1)}, u32[]{:S(2)}, u32[]{:S(2)}) collective-permute-start(f32[4,10,1,128]{3,1,2,0:T(8,128)S(1)} %get-tuple-element.34), channel_id=1, source_target_pairs={{2,0},{4,2},{6,4},{3,1},{5,3},{7,5},{10,8},{12,10},{14,12},{11,9},... | collective-permute-start | bytes 61448 | tf_op jit(solution)/shard_map/ppermute | solution.py:20
  52.9 6.1 %collective-permute-start.3 = (f32[4,10,1,128]{3,1,2,0:T(8,128)S(1)}, f32[4,10,1,128]{3,1,2,0:T(8,128)S(1)}, u32[]{:S(2)}, u32[]{:S(2)}) collective-permute-start(f32[4,10,1,128]{3,1,2,0:T(8,128)S(1)} %get-tuple-element.33), channel_id=1, source_target_pairs={{0,2},{2,4},{4,6},{1,3},{3,5},{5,7},{8,10},{10,12},{12,14},{9,11},... | collective-permute-start | bytes 61448 | tf_op jit(solution)/shard_map/ppermute | solution.py:17
  59.1 6.1 %copy-start.2 = (f32[8,8,128]{2,1,0:T(8,128)S(1)}, f32[8,8,128]{2,1,0:T(8,128)}, u32[]{:S(2)}) copy-start(f32[8,8,128]{2,1,0:T(8,128)} %param.7) | copy-start | bytes 98308
  59.1 13.6 %copy-start.3 = (f32[4,8,8,128]{3,2,1,0:T(8,128)S(1)}, f32[4,8,8,128]{3,2,1,0:T(8,128)}, u32[]{:S(2)}) copy-start(f32[4,8,8,128]{3,2,1,0:T(8,128)} %param.5) | copy-start | bytes 393220
  59.3 12.3 %collective-permute-start.4 = (f32[4,10,10,1]{3,1,2,0:T(8,128)S(1)}, f32[4,10,10,1]{3,1,2,0:T(8,128)S(1)}, u32[]{:S(2)}, u32[]{:S(2)}) collective-permute-start(f32[4,10,10,1]{3,1,2,0:T(8,128)S(1)} %get-tuple-element.27), channel_id=1, source_target_pairs={{1,0},{3,2},{5,4},{7,6},{9,8},{11,10},{13,12},{15,14},{17,16},{19,... | collective-permute-start | bytes 4808 | tf_op jit(solution)/shard_map/ppermute | solution.py:20
  60.6 12.2 %collective-permute-start.5 = (f32[4,10,10,1]{3,1,2,0:T(8,128)S(1)}, f32[4,10,10,1]{3,1,2,0:T(8,128)S(1)}, u32[]{:S(2)}, u32[]{:S(2)}) collective-permute-start(f32[4,10,10,1]{3,1,2,0:T(8,128)S(1)} %get-tuple-element.28), channel_id=1, source_target_pairs={{0,1},{2,3},{4,5},{6,7},{8,9},{10,11},{12,13},{14,15},{16,17},{18,... | collective-permute-start | bytes 4808 | tf_op jit(solution)/shard_map/ppermute | solution.py:17
  72.7 0.7 copy-start.4
  73.8 4.3 %collective-permute-start.6 = (f32[4,1,8,128]{3,1,2,0:T(1,128)S(1)}, f32[4,1,8,128]{3,1,2,0:T(1,128)S(1)}, u32[]{:S(2)}, u32[]{:S(2)}) collective-permute-start(f32[4,1,8,128]{3,1,2,0:T(1,128)S(1)} %get-tuple-element.38), channel_id=1, source_target_pairs={{8,0},{16,8},{24,16},{9,1},{17,9},{25,17},{10,2},{18,10},{26,18},{... | collective-permute-start | bytes 49160 | tf_op jit(solution)/shard_map/ppermute | solution.py:20
  75.1 3.9 %collective-permute-start.7 = (f32[4,1,8,128]{3,1,2,0:T(1,128)S(1)}, f32[4,1,8,128]{3,1,2,0:T(1,128)S(1)}, u32[]{:S(2)}, u32[]{:S(2)}) collective-permute-start(f32[4,1,8,128]{3,1,2,0:T(1,128)S(1)} %get-tuple-element.37), channel_id=1, source_target_pairs={{0,8},{8,16},{16,24},{1,9},{9,17},{17,25},{2,10},{10,18},{18,26},{... | collective-permute-start | bytes 49160 | tf_op jit(solution)/shard_map/ppermute | solution.py:17
  79.0 6.1 %collective-permute-start.8 = (f32[4,10,1,128]{3,1,2,0:T(8,128)S(1)}, f32[4,10,1,128]{3,1,2,0:T(8,128)S(1)}, u32[]{:S(2)}, u32[]{:S(2)}) collective-permute-start(f32[4,10,1,128]{3,1,2,0:T(8,128)S(1)} %get-tuple-element.32), channel_id=1, source_target_pairs={{2,0},{4,2},{6,4},{3,1},{5,3},{7,5},{10,8},{12,10},{14,12},{11,9},... | collective-permute-start | bytes 61448 | tf_op jit(solution)/shard_map/ppermute | solution.py:20
  80.3 6.1 %collective-permute-start.9 = (f32[4,10,1,128]{3,1,2,0:T(8,128)S(1)}, f32[4,10,1,128]{3,1,2,0:T(8,128)S(1)}, u32[]{:S(2)}, u32[]{:S(2)}) collective-permute-start(f32[4,10,1,128]{3,1,2,0:T(8,128)S(1)} %get-tuple-element.31), channel_id=1, source_target_pairs={{0,2},{2,4},{4,6},{1,3},{3,5},{5,7},{8,10},{10,12},{12,14},{9,11},... | collective-permute-start | bytes 61448 | tf_op jit(solution)/shard_map/ppermute | solution.py:17
  86.7 11.4 %collective-permute-start.10 = (f32[4,10,10,1]{3,1,2,0:T(8,128)S(1)}, f32[4,10,10,1]{3,1,2,0:T(8,128)S(1)}, u32[]{:S(2)}, u32[]{:S(2)}) collective-permute-start(f32[4,10,10,1]{3,1,2,0:T(8,128)S(1)} %get-tuple-element.25), channel_id=1, source_target_pairs={{1,0},{3,2},{5,4},{7,6},{9,8},{11,10},{13,12},{15,14},{17,16},{19,... | collective-permute-start | bytes 4808 | tf_op jit(solution)/shard_map/ppermute | solution.py:20
  88.0 11.3 %collective-permute-start.11 = (f32[4,10,10,1]{3,1,2,0:T(8,128)S(1)}, f32[4,10,10,1]{3,1,2,0:T(8,128)S(1)}, u32[]{:S(2)}, u32[]{:S(2)}) collective-permute-start(f32[4,10,10,1]{3,1,2,0:T(8,128)S(1)} %get-tuple-element.26), channel_id=1, source_target_pairs={{0,1},{2,3},{4,5},{6,7},{8,9},{10,11},{12,13},{14,15},{16,17},{18,... | collective-permute-start | bytes 4808 | tf_op jit(solution)/shard_map/ppermute | solution.py:17
  141.7 4.9 %collective-permute-start.12 = (f32[4,1,8,128]{3,1,2,0:T(1,128)S(1)}, f32[4,1,8,128]{3,1,2,0:T(1,128)S(1)}, u32[]{:S(2)}, u32[]{:S(2)}) collective-permute-start(f32[4,1,8,128]{3,1,2,0:T(1,128)S(1)} %get-tuple-element.36), channel_id=1, source_target_pairs={{8,0},{16,8},{24,16},{9,1},{17,9},{25,17},{10,2},{18,10},{26,18},{... | collective-permute-start | bytes 49160 | tf_op jit(solution)/shard_map/ppermute | solution.py:20
  143.0 3.9 %collective-permute-start.13 = (f32[4,1,8,128]{3,1,2,0:T(1,128)S(1)}, f32[4,1,8,128]{3,1,2,0:T(1,128)S(1)}, u32[]{:S(2)}, u32[]{:S(2)}) collective-permute-start(f32[4,1,8,128]{3,1,2,0:T(1,128)S(1)} %get-tuple-element.35), channel_id=1, source_target_pairs={{0,8},{8,16},{16,24},{1,9},{9,17},{17,25},{2,10},{10,18},{18,26},{... | collective-permute-start | bytes 49160 | tf_op jit(solution)/shard_map/ppermute | solution.py:17
  146.9 6.1 %collective-permute-start.14 = (f32[4,10,1,128]{3,1,2,0:T(8,128)S(1)}, f32[4,10,1,128]{3,1,2,0:T(8,128)S(1)}, u32[]{:S(2)}, u32[]{:S(2)}) collective-permute-start(f32[4,10,1,128]{3,1,2,0:T(8,128)S(1)} %get-tuple-element.30), channel_id=1, source_target_pairs={{2,0},{4,2},{6,4},{3,1},{5,3},{7,5},{10,8},{12,10},{14,12},{11,9},... | collective-permute-start | bytes 61448 | tf_op jit(solution)/shard_map/ppermute | solution.py:20
  148.2 6.1 %collective-permute-start.15 = (f32[4,10,1,128]{3,1,2,0:T(8,128)S(1)}, f32[4,10,1,128]{3,1,2,0:T(8,128)S(1)}, u32[]{:S(2)}, u32[]{:S(2)}) collective-permute-start(f32[4,10,1,128]{3,1,2,0:T(8,128)S(1)} %get-tuple-element.29), channel_id=1, source_target_pairs={{0,2},{2,4},{4,6},{1,3},{3,5},{5,7},{8,10},{10,12},{12,14},{9,11},... | collective-permute-start | bytes 61448 | tf_op jit(solution)/shard_map/ppermute | solution.py:17
  154.6 12.3 %collective-permute-start.16 = (f32[4,10,10,1]{3,1,2,0:T(8,128)S(1)}, f32[4,10,10,1]{3,1,2,0:T(8,128)S(1)}, u32[]{:S(2)}, u32[]{:S(2)}) collective-permute-start(f32[4,10,10,1]{3,1,2,0:T(8,128)S(1)} %get-tuple-element.23), channel_id=1, source_target_pairs={{1,0},{3,2},{5,4},{7,6},{9,8},{11,10},{13,12},{15,14},{17,16},{19,... | collective-permute-start | bytes 4808 | tf_op jit(solution)/shard_map/ppermute | solution.py:20
  155.9 12.2 %collective-permute-start.17 = (f32[4,10,10,1]{3,1,2,0:T(8,128)S(1)}, f32[4,10,10,1]{3,1,2,0:T(8,128)S(1)}, u32[]{:S(2)}, u32[]{:S(2)}) collective-permute-start(f32[4,10,10,1]{3,1,2,0:T(8,128)S(1)} %get-tuple-element.24), channel_id=1, source_target_pairs={{0,1},{2,3},{4,5},{6,7},{8,9},{10,11},{12,13},{14,15},{16,17},{18,... | collective-permute-start | bytes 4808 | tf_op jit(solution)/shard_map/ppermute | solution.py:17
where the time goes:
time: 256 us; the launch traced here: 255 us
  blocking collectives  165 us (64%)
  starting transfers between devices  48.1 us (19%)
  waiting for transfers between devices  26.6 us (10%)
  matrix products  9.83 us (4%)
  local copies, waits for them, and re-layouts  2.59 us (1%)
    psum x2, blocking collectives, on_device(): norm_now, curvature = lax.psum((norm_part, curv_part), ('gx', 'gy', 'gz'))  83.3 us
    psum x1, blocking collectives, on_device(): coef_sum, gram_sum = lax.psum((local_coef, local_gram), ('gx', 'gy', 'gz'))  41.9 us
    psum x1, blocking collectives, on_device(): lax.psum((project(iterate), jnp.sum(iterate * iterate, axis=(1, 2, 3))),...  40.1 us
    ppermute x9, starting transfers between devices, padded_2(): lax.ppermute(lax.slice_in_dim(block, block.shape[dim] - width, None, axis...  36.5 us
    ppermute x9, waiting for transfers between devices, padded_2(): lax.ppermute(lax.slice_in_dim(block, 0, width, axis=dim), axis, backward)  17.7 us
    ppermute x9, starting transfers between devices, padded_2(): lax.ppermute(lax.slice_in_dim(block, 0, width, axis=dim), axis, backward)  11.6 us
    ppermute x9, waiting for transfers between devices, padded_2(): lax.ppermute(lax.slice_in_dim(block, block.shape[dim] - width, None, axis...  8.87 us
  transfers between devices with their start and end apart: 18, of which 11 were waited for; matrix products, arithmetic and copies ran while one was open for 1% of the time, Pallas kernels for 0%

commit v1 on v0

--- a/solution.py
+++ b/solution.py
@@ -131,7 +131,7 @@
         norm_old = norm_now
         step_old = step_size
     final_moment, final_square = lax.psum(
-        (project(iterate), jnp.sum(iterate * iterate, axis=(1, 2, 3))), ("gx", "gy", "gz")
+        lax.psum((project(iterate), jnp.sum(iterate * iterate, axis=(1, 2, 3))), ("gy", "gz")), "gx"
     )
     weights = final_moment / point_count
     square = final_square / point_count

time: 256 us -> 242 us (0.945)
  blocking collectives: 165 us -> 152 us
    psum x1, blocking collectives: 40.1 us -> 21.1 us  [on_device(): lax.psum((project(iterate), jnp.sum(iterate * iterate, axis=(1, 2, 3))),...]
    psum x0 -> x1, blocking collectives: none -> 5.65 us  [on_device(): lax.psum(lax.psum((project(iterate), jnp.sum(iterate * iterate, axis=(1,...]
where the time goes in v1:
time: 242 us; the launch traced here: 241 us
  blocking collectives  152 us (63%)
  starting transfers between devices  48.1 us (20%)
  waiting for transfers between devices  26.6 us (11%)
  matrix products  9.83 us (4%)
  local copies, waits for them, and re-layouts  2.59 us (1%)
    psum x2, blocking collectives, on_device(): norm_now, curvature = lax.psum((norm_part, curv_part), ('gx', 'gy', 'gz'))  83.5 us
    psum x1, blocking collectives, on_device(): coef_sum, gram_sum = lax.psum((local_coef, local_gram), ('gx', 'gy', 'gz'))  41.9 us
    ppermute x9, starting transfers between devices, padded_2(): lax.ppermute(lax.slice_in_dim(block, block.shape[dim] - width, None, axis...  36.5 us
    psum x1, blocking collectives, on_device(): lax.psum((project(iterate), jnp.sum(iterate * iterate, axis=(1, 2, 3))),...  21.1 us
    ppermute x9, waiting for transfers between devices, padded_2(): lax.ppermute(lax.slice_in_dim(block, 0, width, axis=dim), axis, backward)  17.7 us
    ppermute x9, starting transfers between devices, padded_2(): lax.ppermute(lax.slice_in_dim(block, 0, width, axis=dim), axis, backward)  11.6 us
    ppermute x9, waiting for transfers between devices, padded_2(): lax.ppermute(lax.slice_in_dim(block, block.shape[dim] - width, None, axis...  8.87 us
    psum x1, blocking collectives, on_device(): lax.psum(lax.psum((project(iterate), jnp.sum(iterate * iterate, axis=(1,...  5.65 us
  transfers between devices with their start and end apart: 18, of which 11 were waited for; matrix products, arithmetic and copies ran while one was open for 1% of the time, Pallas kernels for 0%

profile of v1, /device:TPU:0, one launch (start us, length us, event | category | flops | bytes accessed | tf_op | source)
XLA Modules:
  0.0 241.3 jit_solution(6364068892591150914)
XLA Ops:
  0.7 2.6 %fusion.20 = f32[4,1,8,1,1]{2,1,4,3,0:T(1,128)S(1)} fusion(f32[4,8,8,128,1]{3,4,2,1,0:T(1,128)} %bitcast.131, bf16[4,8,8,8,128]{4,3,2,1,0:T(8,128)(2,1)} %param.6), kind=kOutput, calls=%fused_computation.31 | convolution fusion | flops 3145728 | bytes 655488 | tf_op jit(solution)/shard_map/skxyz,sxyz->sk/dot_general | solution.py:95
  3.3 41.9 %psum.70 = f32[4,8]{1,0:T(4,128)S(1)} all-reduce(f32[4,8]{1,0:T(4,128)S(1)} %bitcast.130), channel_id=1, replica_groups=mesh['gx'=4,'gy'=4,'gz'=2] {'gx','gy','gz'}, use_global_device_ids=true, to_apply=%region_0.1 | all-reduce | flops 32 | bytes 256 | tf_op jit(solution)/shard_map/psum | solution.py:102
  47.3 3.0 %collective-permute-start.1 = (f32[4,1,8,128]{3,1,2,0:T(1,128)S(1)}, f32[4,1,8,128]{3,1,2,0:T(1,128)S(1)}, u32[]{:S(2)}, u32[]{:S(2)}) collective-permute-start(f32[4,1,8,128]{3,1,2,0:T(1,128)S(1)} %get-tuple-element.41), channel_id=1, source_target_pairs={{0,8},{8,16},{16,24},{1,9},{9,17},{17,25},{2,10},{10,18},{18,26},{... | collective-permute-start | bytes 49160 | tf_op jit(solution)/shard_map/ppermute | solution.py:17
  51.6 1.3 collective-permute-start.2
  52.9 4.5 %collective-permute-start.3 = (f32[4,10,1,128]{3,1,2,0:T(8,128)S(1)}, f32[4,10,1,128]{3,1,2,0:T(8,128)S(1)}, u32[]{:S(2)}, u32[]{:S(2)}) collective-permute-start(f32[4,10,1,128]{3,1,2,0:T(8,128)S(1)} %get-tuple-element.35), channel_id=1, source_target_pairs={{0,2},{2,4},{4,6},{1,3},{3,5},{5,7},{8,10},{10,12},{12,14},{9,11},... | collective-permute-start | bytes 61448 | tf_op jit(solution)/shard_map/ppermute | solution.py:17
  57.5 1.6 collective-permute-done.3
  60.6 4.6 %collective-permute-start.5 = (f32[4,10,10,1]{3,1,2,0:T(8,128)S(1)}, f32[4,10,10,1]{3,1,2,0:T(8,128)S(1)}, u32[]{:S(2)}, u32[]{:S(2)}) collective-permute-start(f32[4,10,10,1]{3,1,2,0:T(8,128)S(1)} %get-tuple-element.30), channel_id=1, source_target_pairs={{0,1},{2,3},{4,5},{6,7},{8,9},{10,11},{12,13},{14,15},{16,17},{18,... | collective-permute-start | bytes 4808 | tf_op jit(solution)/shard_map/ppermute | solution.py:17
  65.2 6.3 %collective-permute-done.4 = f32[4,10,10,1]{3,1,2,0:T(8,128)S(1)} collective-permute-done((f32[4,10,10,1]{3,1,2,0:T(8,128)S(1)}, f32[4,10,10,1]{3,1,2,0:T(8,128)S(1)}, u32[]{:S(2)}, u32[]{:S(2)}) %collective-permute-start.4) | collective-permute-done | bytes 1632 | tf_op jit(solution)/shard_map/ppermute | solution.py:20
  75.1 3.0 %collective-permute-start.7 = (f32[4,1,8,128]{3,1,2,0:T(1,128)S(1)}, f32[4,1,8,128]{3,1,2,0:T(1,128)S(1)}, u32[]{:S(2)}, u32[]{:S(2)}) collective-permute-start(f32[4,1,8,128]{3,1,2,0:T(1,128)S(1)} %get-tuple-element.39), channel_id=1, source_target_pairs={{0,8},{8,16},{16,24},{1,9},{9,17},{17,25},{2,10},{10,18},{18,26},{... | collective-permute-start | bytes 49160 | tf_op jit(solution)/shard_map/ppermute | solution.py:17
  80.3 4.6 %collective-permute-start.9 = (f32[4,10,1,128]{3,1,2,0:T(8,128)S(1)}, f32[4,10,1,128]{3,1,2,0:T(8,128)S(1)}, u32[]{:S(2)}, u32[]{:S(2)}) collective-permute-start(f32[4,10,1,128]{3,1,2,0:T(8,128)S(1)} %get-tuple-element.33), channel_id=1, source_target_pairs={{0,2},{2,4},{4,6},{1,3},{3,5},{5,7},{8,10},{10,12},{12,14},{9,11},... | collective-permute-start | bytes 61448 | tf_op jit(solution)/shard_map/ppermute | solution.py:17
  85.1 1.3 collective-permute-done.9
  88.0 4.6 %collective-permute-start.11 = (f32[4,10,10,1]{3,1,2,0:T(8,128)S(1)}, f32[4,10,10,1]{3,1,2,0:T(8,128)S(1)}, u32[]{:S(2)}, u32[]{:S(2)}) collective-permute-start(f32[4,10,10,1]{3,1,2,0:T(8,128)S(1)} %get-tuple-element.28), channel_id=1, source_target_pairs={{0,1},{2,3},{4,5},{6,7},{8,9},{10,11},{12,13},{14,15},{16,17},{18,... | collective-permute-start | bytes 4808 | tf_op jit(solution)/shard_map/ppermute | solution.py:17
  92.8 5.2 %collective-permute-done.10 = f32[4,10,10,1]{3,1,2,0:T(8,128)S(1)} collective-permute-done((f32[4,10,10,1]{3,1,2,0:T(8,128)S(1)}, f32[4,10,10,1]{3,1,2,0:T(8,128)S(1)}, u32[]{:S(2)}, u32[]{:S(2)}) %collective-permute-start.10) | collective-permute-done | bytes 1632 | tf_op jit(solution)/shard_map/ppermute | solution.py:20
  99.7 41.8 %all-reduce.1 = (f32[4]{0:T(128)S(1)}, f32[4]{0:T(128)S(1)}) all-reduce(f32[4]{0:T(128)S(1)} %get-tuple-element.7, f32[4]{0:T(128)S(1)} %get-tuple-element.6), channel_id=1, replica_groups=mesh['gx'=4,'gy'=4,'gz'=2] {'gx','gy','gz'}, use_global_device_ids=true, to_apply=%region_2.3 | all-reduce | flops 8 | bytes 64 | tf_op jit(solution)/shard_map/psum | solution.py:117
  141.7 1.3 collective-permute-start.12
  143.0 3.0 %collective-permute-start.13 = (f32[4,1,8,128]{3,1,2,0:T(1,128)S(1)}, f32[4,1,8,128]{3,1,2,0:T(1,128)S(1)}, u32[]{:S(2)}, u32[]{:S(2)}) collective-permute-start(f32[4,1,8,128]{3,1,2,0:T(1,128)S(1)} %get-tuple-element.37), channel_id=1, source_target_pairs={{0,8},{8,16},{16,24},{1,9},{9,17},{17,25},{2,10},{10,18},{18,26},{... | collective-permute-start | bytes 49160 | tf_op jit(solution)/shard_map/ppermute | solution.py:17
  148.2 4.5 %collective-permute-start.15 = (f32[4,10,1,128]{3,1,2,0:T(8,128)S(1)}, f32[4,10,1,128]{3,1,2,0:T(8,128)S(1)}, u32[]{:S(2)}, u32[]{:S(2)}) collective-permute-start(f32[4,10,1,128]{3,1,2,0:T(8,128)S(1)} %get-tuple-element.31), channel_id=1, source_target_pairs={{0,2},{2,4},{4,6},{1,3},{3,5},{5,7},{8,10},{10,12},{12,14},{9,11},... | collective-permute-start | bytes 61448 | tf_op jit(solution)/shard_map/ppermute | solution.py:17
  153.0 1.3 collective-permute-done.15
  155.9 4.6 %collective-permute-start.17 = (f32[4,10,10,1]{3,1,2,0:T(8,128)S(1)}, f32[4,10,10,1]{3,1,2,0:T(8,128)S(1)}, u32[]{:S(2)}, u32[]{:S(2)}) collective-permute-start(f32[4,10,10,1]{3,1,2,0:T(8,128)S(1)} %get-tuple-element.26), channel_id=1, source_target_pairs={{0,1},{2,3},{4,5},{6,7},{8,9},{10,11},{12,13},{14,15},{16,17},{18,... | collective-permute-start | bytes 4808 | tf_op jit(solution)/shard_map/ppermute | solution.py:17
  160.7 6.1 %collective-permute-done.16 = f32[4,10,10,1]{3,1,2,0:T(8,128)S(1)} collective-permute-done((f32[4,10,10,1]{3,1,2,0:T(8,128)S(1)}, f32[4,10,10,1]{3,1,2,0:T(8,128)S(1)}, u32[]{:S(2)}, u32[]{:S(2)}) %collective-permute-start.16) | collective-permute-done | bytes 1632 | tf_op jit(solution)/shard_map/ppermute | solution.py:20
  168.5 41.7 %all-reduce = (f32[4]{0:T(128)S(1)}, f32[4]{0:T(128)S(1)}, f32[4,8,8]{2,1,0:T(8,128)S(1)}) all-reduce(f32[4]{0:T(128)S(1)} %get-tuple-element.23, f32[4]{0:T(128)S(1)} %fusion.11, f32[4,8,8]{2,1,0:T(8,128)S(1)} %convolution_bitcast_fusion.3), channel_id=1, replica_groups=mesh['gx'=4,'gy'=4,'gz'=2] {'gx','gy','gz'}, use_global_device_ids=true, to_apply=%region_6.7 | all-reduce | flops 264 | bytes 2112 | tf_op jit(solution)/shard_map/psum | solution.py:119
  211.2 1.6 fusion.16
  212.8 21.1 %all-reduce.2 = (f32[4,8]{1,0:T(4,128)S(1)}, f32[4]{0:T(128)S(1)}) all-reduce(f32[4,8]{1,0:T(4,128)S(1)} %bitcast.129, f32[4]{0:T(128)S(1)} %get-tuple-element.19), channel_id=1, replica_groups=mesh['gx'=4,'gy'=4,'gz'=2] {'gy','gz'}, use_global_device_ids=true, to_apply=%region_9.10 | all-reduce | flops 36 | bytes 288 | tf_op jit(solution)/shard_map/psum | solution.py:134
  233.9 5.6 %all-reduce.3 = (f32[4,8]{1,0:T(4,128)S(1)}, f32[4]{0:T(128)S(1)}) all-reduce(f32[4,8]{1,0:T(4,128)S(1)} %get-tuple-element.15, f32[4]{0:T(128)S(1)} %get-tuple-element.16), channel_id=1, replica_groups=mesh['gx'=4,'gy'=4,'gz'=2] {'gx'}, use_global_device_ids=true, to_apply=%region_10.11 | all-reduce | flops 36 | bytes 288 | tf_op jit(solution)/shard_map/psum | solution.py:133
  (75 shorter events, 22.9 us)
Async XLA Ops:
  0.6 49.8 %copy-start = (f32[8,8]{1,0:T(8,128)S(1)}, f32[8,8]{1,0:T(8,128)}, u32[]{:S(2)}) copy-start(f32[8,8]{1,0:T(8,128)} %param.9) | copy-start | bytes 772
  0.6 44.6 %copy-start.1 = (bf16[4,8,8,8,128]{4,3,2,1,0:T(8,128)(2,1)S(1)}, bf16[4,8,8,8,128]{4,3,2,1,0:T(8,128)(2,1)}, u32[]{:S(2)}) copy-start(bf16[4,8,8,8,128]{4,3,2,1,0:T(8,128)(2,1)} %param.6) | copy-start | bytes 1572868
  46.0 5.6 %collective-permute-start = (f32[4,1,8,128]{3,1,2,0:T(1,128)S(1)}, f32[4,1,8,128]{3,1,2,0:T(1,128)S(1)}, u32[]{:S(2)}, u32[]{:S(2)}) collective-permute-start(f32[4,1,8,128]{3,1,2,0:T(1,128)S(1)} %get-tuple-element.42), channel_id=1, source_target_pairs={{8,0},{16,8},{24,16},{9,1},{17,9},{25,17},{10,2},{18,10},{26,18},{... | collective-permute-start | bytes 49160 | tf_op jit(solution)/shard_map/ppermute | solution.py:20
  47.3 4.3 %collective-permute-start.1 = (f32[4,1,8,128]{3,1,2,0:T(1,128)S(1)}, f32[4,1,8,128]{3,1,2,0:T(1,128)S(1)}, u32[]{:S(2)}, u32[]{:S(2)}) collective-permute-start(f32[4,1,8,128]{3,1,2,0:T(1,128)S(1)} %get-tuple-element.41), channel_id=1, source_target_pairs={{0,8},{8,16},{16,24},{1,9},{9,17},{17,25},{2,10},{10,18},{18,26},{... | collective-permute-start | bytes 49160 | tf_op jit(solution)/shard_map/ppermute | solution.py:17
  51.6 5.9 %collective-permute-start.2 = (f32[4,10,1,128]{3,1,2,0:T(8,128)S(1)}, f32[4,10,1,128]{3,1,2,0:T(8,128)S(1)}, u32[]{:S(2)}, u32[]{:S(2)}) collective-permute-start(f32[4,10,1,128]{3,1,2,0:T(8,128)S(1)} %get-tuple-element.36), channel_id=1, source_target_pairs={{2,0},{4,2},{6,4},{3,1},{5,3},{7,5},{10,8},{12,10},{14,12},{11,9},... | collective-permute-start | bytes 61448 | tf_op jit(solution)/shard_map/ppermute | solution.py:20
  52.9 6.1 %collective-permute-start.3 = (f32[4,10,1,128]{3,1,2,0:T(8,128)S(1)}, f32[4,10,1,128]{3,1,2,0:T(8,128)S(1)}, u32[]{:S(2)}, u32[]{:S(2)}) collective-permute-start(f32[4,10,1,128]{3,1,2,0:T(8,128)S(1)} %get-tuple-element.35), channel_id=1, source_target_pairs={{0,2},{2,4},{4,6},{1,3},{3,5},{5,7},{8,10},{10,12},{12,14},{9,11},... | collective-permute-start | bytes 61448 | tf_op jit(solution)/shard_map/ppermute | solution.py:17
  59.1 6.1 %copy-start.2 = (f32[8,8,128]{2,1,0:T(8,128)S(1)}, f32[8,8,128]{2,1,0:T(8,128)}, u32[]{:S(2)}) copy-start(f32[8,8,128]{2,1,0:T(8,128)} %param.7) | copy-start | bytes 98308
  59.1 13.6 %copy-start.3 = (f32[4,8,8,128]{3,2,1,0:T(8,128)S(1)}, f32[4,8,8,128]{3,2,1,0:T(8,128)}, u32[]{:S(2)}) copy-start(f32[4,8,8,128]{3,2,1,0:T(8,128)} %param.5) | copy-start | bytes 393220
  59.3 12.3 %collective-permute-start.4 = (f32[4,10,10,1]{3,1,2,0:T(8,128)S(1)}, f32[4,10,10,1]{3,1,2,0:T(8,128)S(1)}, u32[]{:S(2)}, u32[]{:S(2)}) collective-permute-start(f32[4,10,10,1]{3,1,2,0:T(8,128)S(1)} %get-tuple-element.29), channel_id=1, source_target_pairs={{1,0},{3,2},{5,4},{7,6},{9,8},{11,10},{13,12},{15,14},{17,16},{19,... | collective-permute-start | bytes 4808 | tf_op jit(solution)/shard_map/ppermute | solution.py:20
  60.6 12.2 %collective-permute-start.5 = (f32[4,10,10,1]{3,1,2,0:T(8,128)S(1)}, f32[4,10,10,1]{3,1,2,0:T(8,128)S(1)}, u32[]{:S(2)}, u32[]{:S(2)}) collective-permute-start(f32[4,10,10,1]{3,1,2,0:T(8,128)S(1)} %get-tuple-element.30), channel_id=1, source_target_pairs={{0,1},{2,3},{4,5},{6,7},{8,9},{10,11},{12,13},{14,15},{16,17},{18,... | collective-permute-start | bytes 4808 | tf_op jit(solution)/shard_map/ppermute | solution.py:17
  72.7 0.7 copy-start.4
  73.8 4.3 %collective-permute-start.6 = (f32[4,1,8,128]{3,1,2,0:T(1,128)S(1)}, f32[4,1,8,128]{3,1,2,0:T(1,128)S(1)}, u32[]{:S(2)}, u32[]{:S(2)}) collective-permute-start(f32[4,1,8,128]{3,1,2,0:T(1,128)S(1)} %get-tuple-element.40), channel_id=1, source_target_pairs={{8,0},{16,8},{24,16},{9,1},{17,9},{25,17},{10,2},{18,10},{26,18},{... | collective-permute-start | bytes 49160 | tf_op jit(solution)/shard_map/ppermute | solution.py:20
  75.1 3.9 %collective-permute-start.7 = (f32[4,1,8,128]{3,1,2,0:T(1,128)S(1)}, f32[4,1,8,128]{3,1,2,0:T(1,128)S(1)}, u32[]{:S(2)}, u32[]{:S(2)}) collective-permute-start(f32[4,1,8,128]{3,1,2,0:T(1,128)S(1)} %get-tuple-element.39), channel_id=1, source_target_pairs={{0,8},{8,16},{16,24},{1,9},{9,17},{17,25},{2,10},{10,18},{18,26},{... | collective-permute-start | bytes 49160 | tf_op jit(solution)/shard_map/ppermute | solution.py:17
  79.0 6.1 %collective-permute-start.8 = (f32[4,10,1,128]{3,1,2,0:T(8,128)S(1)}, f32[4,10,1,128]{3,1,2,0:T(8,128)S(1)}, u32[]{:S(2)}, u32[]{:S(2)}) collective-permute-start(f32[4,10,1,128]{3,1,2,0:T(8,128)S(1)} %get-tuple-element.34), channel_id=1, source_target_pairs={{2,0},{4,2},{6,4},{3,1},{5,3},{7,5},{10,8},{12,10},{14,12},{11,9},... | collective-permute-start | bytes 61448 | tf_op jit(solution)/shard_map/ppermute | solution.py:20
  80.3 6.1 %collective-permute-start.9 = (f32[4,10,1,128]{3,1,2,0:T(8,128)S(1)}, f32[4,10,1,128]{3,1,2,0:T(8,128)S(1)}, u32[]{:S(2)}, u32[]{:S(2)}) collective-permute-start(f32[4,10,1,128]{3,1,2,0:T(8,128)S(1)} %get-tuple-element.33), channel_id=1, source_target_pairs={{0,2},{2,4},{4,6},{1,3},{3,5},{5,7},{8,10},{10,12},{12,14},{9,11},... | collective-permute-start | bytes 61448 | tf_op jit(solution)/shard_map/ppermute | solution.py:17
  86.7 11.4 %collective-permute-start.10 = (f32[4,10,10,1]{3,1,2,0:T(8,128)S(1)}, f32[4,10,10,1]{3,1,2,0:T(8,128)S(1)}, u32[]{:S(2)}, u32[]{:S(2)}) collective-permute-start(f32[4,10,10,1]{3,1,2,0:T(8,128)S(1)} %get-tuple-element.27), channel_id=1, source_target_pairs={{1,0},{3,2},{5,4},{7,6},{9,8},{11,10},{13,12},{15,14},{17,16},{19,... | collective-permute-start | bytes 4808 | tf_op jit(solution)/shard_map/ppermute | solution.py:20
  88.0 11.3 %collective-permute-start.11 = (f32[4,10,10,1]{3,1,2,0:T(8,128)S(1)}, f32[4,10,10,1]{3,1,2,0:T(8,128)S(1)}, u32[]{:S(2)}, u32[]{:S(2)}) collective-permute-start(f32[4,10,10,1]{3,1,2,0:T(8,128)S(1)} %get-tuple-element.28), channel_id=1, source_target_pairs={{0,1},{2,3},{4,5},{6,7},{8,9},{10,11},{12,13},{14,15},{16,17},{18,... | collective-permute-start | bytes 4808 | tf_op jit(solution)/shard_map/ppermute | solution.py:17
  141.7 4.9 %collective-permute-start.12 = (f32[4,1,8,128]{3,1,2,0:T(1,128)S(1)}, f32[4,1,8,128]{3,1,2,0:T(1,128)S(1)}, u32[]{:S(2)}, u32[]{:S(2)}) collective-permute-start(f32[4,1,8,128]{3,1,2,0:T(1,128)S(1)} %get-tuple-element.38), channel_id=1, source_target_pairs={{8,0},{16,8},{24,16},{9,1},{17,9},{25,17},{10,2},{18,10},{26,18},{... | collective-permute-start | bytes 49160 | tf_op jit(solution)/shard_map/ppermute | solution.py:20
  143.0 3.9 %collective-permute-start.13 = (f32[4,1,8,128]{3,1,2,0:T(1,128)S(1)}, f32[4,1,8,128]{3,1,2,0:T(1,128)S(1)}, u32[]{:S(2)}, u32[]{:S(2)}) collective-permute-start(f32[4,1,8,128]{3,1,2,0:T(1,128)S(1)} %get-tuple-element.37), channel_id=1, source_target_pairs={{0,8},{8,16},{16,24},{1,9},{9,17},{17,25},{2,10},{10,18},{18,26},{... | collective-permute-start | bytes 49160 | tf_op jit(solution)/shard_map/ppermute | solution.py:17
  146.9 6.1 %collective-permute-start.14 = (f32[4,10,1,128]{3,1,2,0:T(8,128)S(1)}, f32[4,10,1,128]{3,1,2,0:T(8,128)S(1)}, u32[]{:S(2)}, u32[]{:S(2)}) collective-permute-start(f32[4,10,1,128]{3,1,2,0:T(8,128)S(1)} %get-tuple-element.32), channel_id=1, source_target_pairs={{2,0},{4,2},{6,4},{3,1},{5,3},{7,5},{10,8},{12,10},{14,12},{11,9},... | collective-permute-start | bytes 61448 | tf_op jit(solution)/shard_map/ppermute | solution.py:20
  148.2 6.1 %collective-permute-start.15 = (f32[4,10,1,128]{3,1,2,0:T(8,128)S(1)}, f32[4,10,1,128]{3,1,2,0:T(8,128)S(1)}, u32[]{:S(2)}, u32[]{:S(2)}) collective-permute-start(f32[4,10,1,128]{3,1,2,0:T(8,128)S(1)} %get-tuple-element.31), channel_id=1, source_target_pairs={{0,2},{2,4},{4,6},{1,3},{3,5},{5,7},{8,10},{10,12},{12,14},{9,11},... | collective-permute-start | bytes 61448 | tf_op jit(solution)/shard_map/ppermute | solution.py:17
  154.6 12.3 %collective-permute-start.16 = (f32[4,10,10,1]{3,1,2,0:T(8,128)S(1)}, f32[4,10,10,1]{3,1,2,0:T(8,128)S(1)}, u32[]{:S(2)}, u32[]{:S(2)}) collective-permute-start(f32[4,10,10,1]{3,1,2,0:T(8,128)S(1)} %get-tuple-element.25), channel_id=1, source_target_pairs={{1,0},{3,2},{5,4},{7,6},{9,8},{11,10},{13,12},{15,14},{17,16},{19,... | collective-permute-start | bytes 4808 | tf_op jit(solution)/shard_map/ppermute | solution.py:20
  155.9 12.2 %collective-permute-start.17 = (f32[4,10,10,1]{3,1,2,0:T(8,128)S(1)}, f32[4,10,10,1]{3,1,2,0:T(8,128)S(1)}, u32[]{:S(2)}, u32[]{:S(2)}) collective-permute-start(f32[4,10,10,1]{3,1,2,0:T(8,128)S(1)} %get-tuple-element.26), channel_id=1, source_target_pairs={{0,1},{2,3},{4,5},{6,7},{8,9},{10,11},{12,13},{14,15},{16,17},{18,... | collective-permute-start | bytes 4808 | tf_op jit(solution)/shard_map/ppermute | solution.py:17
